TPU v7x, 128 devices: a whole 4x4x4 slice. The times are simulated.
128 devices in a mesh: depth: 8 (over y, core), lat: 16 (over z, x).
Axes of the slice: x: 4, y: 4, z: 4, core: 2. Of those that a mesh axis runs over, the one named last changes fastest.
Arguments:
- emission: float32 [1024, 16, 2048], P('depth', None, 'lat'), may hold values from 0 to 2
- absorption: float32 [1024, 16, 2048], P('depth', None, 'lat'), may hold values from -4 to 4
- target: float32 [3, 16, 2048], P(None, None, 'lat'), may hold values from 0.2 to 0.8
- shift_whole: int32 [3, 1024], P(None, 'depth'), may hold values from -30 to 30, as said below
- shift_fraction: int32 [3, 1024], P(None, 'depth'), may hold values from 0 to 7, as said below
- taps_table: float32 [8, 4], replicated, may hold values from 0.05 to 0.45
Outputs:
- fitted_emission: float32 [1024, 16, 2048], P('depth', None, 'lat')
- fitted_absorption: float32 [1024, 16, 2048], P('depth', None, 'lat')
Inputs may be any that keep to these rules, and one draw needn't show every extreme that they name: `shift_whole`: both ends of the range are taken in every draw. `shift_fraction`: every value of the range is taken in every draw.
All inputs are finite; a program needn't handle non-finite values.
Results may differ from a plain program's by a relative error of at most 0.0003.
Values sent between devices are 32-bit elements; how exact they have to be, the bound alone decides.
No kernel may reach another device: no remote copies, remote signals or barrier semaphores. Data moves between devices by JAX's collectives and lax.ppermute only.
A program may use at most 128 MiB of HBM per device.

v0:
```python
import jax
import jax.numpy as jnp
from jax import lax
from jax.sharding import PartitionSpec as P

REACH = 32
ITERS = 3
HIGHEST = lax.Precision.HIGHEST
LEARN_RATE = 0.1
BETA_FIRST = 0.9
BETA_SECOND = 0.999
ADAM_EPSILON = 0.001


def copy_for_each(x, axis):
    devices = lax.axis_size(axis)
    return lax.all_to_all(jnp.broadcast_to(x[None], (devices, *x.shape)), axis, 0, 0, tiled=True)


def all_in_one(x, axis):
    leaves = jax.tree.leaves(x)
    sequence = sorted(range(len(leaves)), key=lambda k: -leaves[k].size)
    width = (1, *leaves[sequence[0]].shape)[-1]
    lines = [
        jnp.pad(leaves[k].reshape(-1), (0, -leaves[k].size % width)).reshape(-1, width)
        for k in sequence
    ]
    both, at, found = (copy_for_each(jnp.concatenate(lines), axis), 0, {})
    for k, line in zip(sequence, lines):
        slab = both[:, at : at + len(line)].reshape(len(both), -1)
        found[k] = slab[:, : leaves[k].size].reshape(-1, *leaves[k].shape)
        at += len(line)
    numbers = iter(range(len(leaves)))
    return jax.tree.map(lambda _: found[next(numbers)], x)


def once_a_type(x, axis):
    leaves, found = (jax.tree.leaves(x), {})
    for leading, a in enumerate(leaves):
        if leading not in found:
            alike = [k for k, b in enumerate(leaves) if b.dtype == a.dtype]
            got = (
                all_in_one([leaves[k] for k in alike], axis)
                if len(alike) > 1
                else [copy_for_each(a, axis)]
            )
            for k, b in zip(alike, got):
                found[k] = b
    numbers = iter(range(len(leaves)))
    return jax.tree.map(lambda _: found[next(numbers)], x)


def combined_pairwise(pieces, combine):
    while len(jax.tree.leaves(pieces)[0]) > 1:
        pieces = jax.vmap(combine)(
            *(jax.tree.map(lambda part: part[side::2], pieces) for side in (0, 1))
        )
    return jax.tree.map(lambda part: part[0], pieces)


def carried_in(x, axis, combine, identity, reverse):
    devices, here = (lax.axis_size(axis), lax.axis_index(axis))
    passed = jnp.arange(devices) > here if reverse else jnp.arange(devices) < here

    def kept(part, zero, own):
        part = jnp.where(
            passed.reshape(-1, *(1 for _ in own.shape)), part, jnp.asarray(zero, own.dtype)
        )
        return part[::-1] if reverse else part

    pieces = once_a_type(x, axis)
    return combined_pairwise(jax.tree.map(kept, pieces, identity, x), combine)


def plane_taps(fractions, taps_table):
    levels = jnp.arange(taps_table.shape[0], dtype=jnp.int32)
    picks = (fractions[:, None] == levels[None, :]).astype(jnp.float32)
    return jnp.dot(picks, taps_table, precision=HIGHEST)


def build_band(offsets, tap_weights, tile_width):
    source = jnp.arange(tile_width + 2 * REACH, dtype=jnp.int32)[None, :, None]
    column = jnp.arange(tile_width, dtype=jnp.int32)[None, None, :]
    lag_taps = source - column - REACH - offsets[:, None, None] + 1
    banded = jnp.zeros((offsets.shape[0], tile_width + 2 * REACH, tile_width), jnp.float32)
    for tap_index in range(tap_weights.shape[1]):
        banded = banded + jnp.where(
            lag_taps == tap_index, tap_weights[:, tap_index][:, None, None], 0.0
        )
    return banded


def combine_front(earlier, later):
    return (earlier[0] + jnp.exp(-earlier[1]) * later[0], earlier[1] + later[1])


def combine_back(earlier, later):
    return (later[0] + jnp.exp(-later[1]) * earlier[0], earlier[1] + later[1])


def with_margins(fields):
    blank = jnp.zeros(fields.shape[:3] + (1, REACH), jnp.float32)
    left_part = jnp.concatenate([blank, fields[:, :, :, :-1, -REACH:]], axis=3)
    right_part = jnp.concatenate([fields[:, :, :, 1:, :REACH], blank], axis=3)
    widened = jnp.concatenate([left_part, fields, right_part], axis=4)
    return widened


def fold_margins(spread, tile_width):
    left_rim = spread[:, :, :, :, :REACH]
    right_rim = spread[:, :, :, :, tile_width + REACH :]
    centre = spread[:, :, :, :, REACH : tile_width + REACH]
    blank = jnp.zeros(left_rim.shape[:3] + (1, REACH), jnp.float32)
    from_right = jnp.concatenate([left_rim[:, :, :, 1:], blank], axis=3)
    from_left = jnp.concatenate([blank, right_rim[:, :, :, :-1]], axis=3)
    spacing = ((0, 0), (0, 0), (0, 0), (0, 0))
    tail_part = jnp.pad(from_right, spacing + ((tile_width - REACH, 0),))
    head_part = jnp.pad(from_left, spacing + ((0, tile_width - REACH),))
    return centre + head_part + tail_part


def body(emission, absorption, target, shift_whole, shift_fraction, taps_table):
    tile_width = emission.shape[2]
    total_planes = emission.shape[0] * lax.axis_size("depth")
    fields = jnp.stack([emission, absorption])
    tile_count = lax.axis_size("lat")
    fields, goals = (
        lax.all_to_all(fields, "lat", split_axis=2, concat_axis=3, tiled=True),
        lax.all_to_all(target[None], "lat", split_axis=2, concat_axis=3, tiled=True),
    )
    fields = fields.reshape(fields.shape[:3] + (tile_count, tile_width))
    goals = goals[0].reshape(goals.shape[1:3] + (tile_count, tile_width))
    first_moment = jnp.zeros_like(fields)
    second_moment = jnp.zeros_like(fields)
    for view_index in range(ITERS):
        tap_weights = plane_taps(shift_fraction[view_index], taps_table)
        banded = build_band(shift_whole[view_index], tap_weights, tile_width)
        sheared = jnp.einsum("czrtj,zjx->czrtx", with_margins(fields), banded, precision=HIGHEST)
        color_raw = sheared[0]
        density = sheared[1]
        optical = jax.nn.softplus(density) / total_planes
        transmit_local = jnp.exp(optical - jnp.cumsum(optical, axis=0))
        opacity = -jnp.expm1(-optical)
        emitted = transmit_local * opacity * color_raw
        slab_light = jnp.sum(emitted, axis=0)
        slab_depth = jnp.sum(optical, axis=0)
        blank = jnp.zeros_like(slab_light)
        front_light, front_depth = carried_in(
            (slab_light, slab_depth), "depth", combine_front, (blank, blank), False
        )
        attenuate = jnp.exp(-front_depth)
        back_light, back_depth = carried_in(
            (slab_light, slab_depth), "depth", combine_back, (blank, blank), True
        )
        rendered = front_light + attenuate * (slab_light + jnp.exp(-slab_depth) * back_light)
        residual = rendered - goals[view_index]
        transmit = attenuate * transmit_local
        behind = rendered - front_light - attenuate * jnp.cumsum(emitted, axis=0)
        grad_color = total_planes * residual * transmit * opacity
        grad_density = (
            residual * (transmit * jnp.exp(-optical) * color_raw - behind) * jax.nn.sigmoid(density)
        )
        spread = jnp.einsum(
            "czrtx,zjx->czrtj", jnp.stack([grad_color, grad_density]), banded, precision=HIGHEST
        )
        gradient = fold_margins(spread, tile_width)
        step_number = view_index + 1
        first_moment = BETA_FIRST * first_moment + (1.0 - BETA_FIRST) * gradient
        second_moment = BETA_SECOND * second_moment + (1.0 - BETA_SECOND) * gradient * gradient
        scaled_first = first_moment / (1.0 - BETA_FIRST**step_number)
        scaled_second = second_moment / (1.0 - BETA_SECOND**step_number)
        fields = fields - LEARN_RATE * scaled_first / (jnp.sqrt(scaled_second) + ADAM_EPSILON)
    fields = fields.reshape(fields.shape[:3] + (fields.shape[3] * tile_width,))
    fields = lax.all_to_all(fields, "lat", split_axis=3, concat_axis=2, tiled=True)
    return (fields[0], fields[1])


def solution(mesh):
    in_specs = (
        P("depth", None, "lat"),
        P("depth", None, "lat"),
        P(None, None, "lat"),
        P(None, "depth"),
        P(None, "depth"),
        P(),
    )
    out_specs = (P("depth", None, "lat"), P("depth", None, "lat"))
    return jax.shard_map(body, mesh=mesh, in_specs=in_specs, out_specs=out_specs, check_vma=False)
```

profile of v0, /device:TPU:0, one launch (start us, length us, event | category | flops | bytes accessed | tf_op | source)
XLA Modules:
  0.0 288.7 jit_solution(7464354828743110071)
XLA Ops:
  0.6 1.6 copy.199
  2.2 1.6 copy.200
  3.8 3.2 %pad_maximum_fusion = f32[2,128,16,128]{3,0,1,2:T(2,128)} fusion(f32[1,128,16,128]{3,0,1,2:T(1,128)S(1)} %bitcast.608, f32[1,128,16,128]{3,0,1,2:T(1,128)S(1)} %bitcast.607), kind=kLoop, calls=%fused_computation.74 | loop fusion | flops 524288 | bytes 4194304 | tf_op jit(solution)/shard_map/stack | solution.py:125
  7.0 8.1 %all-to-all-start = ((f32[2,128,16,128]{3,0,1,2:T(2,128)}), f32[2,128,16,128]{3,0,1,2:T(2,128)S(1)}, u32[]{:S(2)}, u32[]{:S(2)}) async-start(f32[2,128,16,128]{3,0,1,2:T(2,128)} %pad_maximum_fusion), calls=%async_computation | async-start | bytes 4194304 | tf_op jit(solution)/shard_map/all_to_all | solution.py:128
  16.6 30.3 %all-to-all-done = f32[2,128,16,128]{3,0,1,2:T(2,128)S(1)} async-done(((f32[2,128,16,128]{3,0,1,2:T(2,128)}), f32[2,128,16,128]{3,0,1,2:T(2,128)S(1)}, u32[]{:S(2)}, u32[]{:S(2)}) %all-to-all-start) | async-done | bytes 2097184 | tf_op jit(solution)/shard_map/all_to_all | solution.py:128
  46.9 3.7 %all-to-all-start.2 = ((f32[1,3,16,128]{3,0,1,2:T(1,128)}), f32[1,3,16,128]{3,0,1,2:T(1,128)S(1)}, u32[]{:S(2)}, u32[]{:S(2)}) async-start(f32[1,3,16,128]{3,0,1,2:T(1,128)} %copy.206), calls=%async_computation.2 | async-start | bytes 49152 | tf_op jit(solution)/shard_map/all_to_all | solution.py:129
  50.6 1.2 copy.280
  52.6 17.9 %fusion.58 = f32[2,128,1,16,128]{4,3,0,1,2:T(8,128)S(1)} fusion(f32[2,128,1,15,32]{4,3,0,1,2:T(8,128)S(1)} %get-tuple-element.37, f32[2,128,1,15,32]{4,3,0,1,2:T(8,128)S(1)} %get-tuple-element.36, f32[2,128,1,16,128]{4,3,0,1,2:T(8,128)S(1)} %bitcast.603, f32[128]{0:T(128)S(1)} %get-tuple-element.115, f32[128]{0:T(128)S(1)} %get-tuple-element.116, ...), kind=kOutput, calls=%fused_computation.91 | convolution fusion | flops 1253572608 | bytes 5278208 | tf_op jit(solution)/shard_map/czrtj,zjx->czrtx/dot_general | solution.py:138
  70.5 1.2 fusion.141
  72.4 4.5 %all-to-all-start.1 = ((f32[8,32,128]{2,1,0:T(8,128)}), f32[8,32,128]{2,1,0:T(8,128)S(1)}, u32[]{:S(2)}, u32[]{:S(2)}) async-start(f32[8,32,128]{2,1,0:T(8,128)} %broadcast_in_dim.227), calls=%async_computation.1 | async-start | bytes 262144 | tf_op jit(solution)/shard_map/all_to_all | solution.py:17
  76.9 6.1 %all-to-all-done.1 = f32[8,32,128]{2,1,0:T(8,128)S(1)} async-done(((f32[8,32,128]{2,1,0:T(8,128)}), f32[8,32,128]{2,1,0:T(8,128)S(1)}, u32[]{:S(2)}, u32[]{:S(2)}) %all-to-all-start.1) | async-done | bytes 131104 | tf_op jit(solution)/shard_map/all_to_all | solution.py:17
  84.4 1.5 fusion.106
  85.9 26.7 %fusion.33 = f32[2,128,1,16,192]{4,3,0,1,2:T(8,128)S(1)} fusion(f32[128]{0:T(128)S(1)} %get-tuple-element.115, f32[128]{0:T(128)S(1)} %get-tuple-element.116, f32[128]{0:T(128)S(1)} %get-tuple-element.117, f32[128]{0:T(128)S(1)} %get-tuple-element.114, s32[128]{0:T(128)S(1)} %get-tuple-element.101, s32[192,128]{1,0:T(8,128)S(1)} %subtract_add_fusion.3, ...), kind=kOutput, calls=%fused_computation.55 | convolution fusion | flops 1249378304 | bytes 5343744 | tf_op jit(solution)/shard_map/czrtx,zjx->czrtj/dot_general | solution.py:163
  114.2 3.8 %divide_subtract_fusion.1 = (f32[2,128,1,16,128]{4,3,0,1,2:T(8,128)S(1)}, f32[2,128,1,16,128]{4,3,0,1,2:T(8,128)}) fusion(f32[2,128,16,128]{3,0,1,2:T(2,128)S(1)} %copy-done.3, f32[2,128,1,15,32]{4,3,0,1,2:T(8,128)S(1)} %get-tuple-element.29, f32[2,128,1,15,32]{4,3,0,1,2:T(8,128)S(1)} %get-tuple-element.28, f32[2,128,1,16,192]{4,3,0,1,2:T(8,128)S(1)} %fusion.33), kind=kLoop, calls=%fused_computation.90 | loop fusion | flops 4718592 | bytes 9371648 | tf_op jit(solution)/shard_map/sub | solution.py:172
  118.8 17.5 %fusion.63 = f32[2,128,1,16,128]{4,3,1,2,0:T(8,128)S(1)} fusion(f32[128]{0:T(128)S(1)} %get-tuple-element.111, f32[128]{0:T(128)S(1)} %get-tuple-element.112, f32[128]{0:T(128)S(1)} %get-tuple-element.113, f32[128]{0:T(128)S(1)} %get-tuple-element.110, s32[128]{0:T(128)S(1)} %get-tuple-element.102, s32[192,128]{1,0:T(8,128)S(1)} %subtract_add_fusion.3, ...), kind=kOutput, calls=%fused_computation.92 | convolution fusion | flops 1253572608 | bytes 5278208 | tf_op jit(solution)/shard_map/czrtj,zjx->czrtx/dot_general | solution.py:138
  136.3 1.2 fusion.92
  138.2 3.4 %all-to-all-start.3 = ((f32[8,32,128]{2,1,0:T(8,128)}), f32[8,32,128]{2,1,0:T(8,128)S(1)}, u32[]{:S(2)}, u32[]{:S(2)}) async-start(f32[8,32,128]{2,1,0:T(8,128)} %broadcast_in_dim.239), calls=%async_computation.3 | async-start | bytes 262144 | tf_op jit(solution)/shard_map/all_to_all | solution.py:17
  141.6 6.0 %all-to-all-done.3 = f32[8,32,128]{2,1,0:T(8,128)S(1)} async-done(((f32[8,32,128]{2,1,0:T(8,128)}), f32[8,32,128]{2,1,0:T(8,128)S(1)}, u32[]{:S(2)}, u32[]{:S(2)}) %all-to-all-start.3) | async-done | bytes 131104 | tf_op jit(solution)/shard_map/all_to_all | solution.py:17
  149.0 1.5 fusion.74
  150.5 26.8 %fusion.36 = f32[2,128,1,16,192]{4,3,0,1,2:T(8,128)S(1)} fusion(f32[128]{0:T(128)S(1)} %get-tuple-element.111, f32[128]{0:T(128)S(1)} %get-tuple-element.112, f32[128]{0:T(128)S(1)} %get-tuple-element.113, f32[128]{0:T(128)S(1)} %get-tuple-element.110, s32[128]{0:T(128)S(1)} %get-tuple-element.102, s32[192,128]{1,0:T(8,128)S(1)} %subtract_add_fusion.3, ...), kind=kOutput, calls=%fused_computation.56 | convolution fusion | flops 1249378304 | bytes 5343744 | tf_op jit(solution)/shard_map/czrtx,zjx->czrtj/dot_general | solution.py:163
  179.6 4.6 %divide_subtract_fusion = f32[2,128,1,16,128]{4,3,0,1,2:T(8,128)S(1)} fusion(f32[2,128,1,16,128]{4,3,0,1,2:T(8,128)S(1)} %copy-done.5, f32[2,128,1,15,32]{4,3,0,1,2:T(8,128)S(1)} %get-tuple-element.27, f32[2,128,1,15,32]{4,3,0,1,2:T(8,128)S(1)} %get-tuple-element.26, f32[2,128,1,16,192]{4,3,0,1,2:T(8,128)S(1)} %fusion.36, f32[2,128,16,128]{3,0,1,2:T(2,128)S(1)} %copy-done.4), kind=kLoop, calls=%fused_computation.88 | loop fusion | flops 11010048 | bytes 9371648 | tf_op jit(solution)/shard_map/sub | solution.py:172
  185.0 17.5 %fusion.68 = f32[2,128,1,16,128]{4,3,1,2,0:T(8,128)S(1)} fusion(f32[128]{0:T(128)S(1)} %get-tuple-element.104, f32[128]{0:T(128)S(1)} %get-tuple-element.105, f32[128]{0:T(128)S(1)} %get-tuple-element.106, f32[128]{0:T(128)S(1)} %get-tuple-element.103, s32[128]{0:T(128)S(1)} %get-tuple-element.100, s32[192,128]{1,0:T(8,128)S(1)} %subtract_add_fusion.3, ...), kind=kOutput, calls=%fused_computation.93 | convolution fusion | flops 1253572608 | bytes 5278208 | tf_op jit(solution)/shard_map/czrtj,zjx->czrtx/dot_general | solution.py:138
  202.5 1.2 fusion.86
  203.7 8.7 %all_to_all.48 = f32[8,32,128]{2,1,0:T(8,128)S(1)} all-to-all(f32[8,32,128]{2,1,0:T(8,128)S(1)} %broadcast_in_dim.248), channel_id=1, replica_groups=mesh['depth'=8,'lat'=16] {'depth'}, dimensions={0} | all-to-all | bytes 262144 | tf_op jit(solution)/shard_map/all_to_all | solution.py:17
  213.8 1.5 fusion.77
  215.3 26.5 %fusion.39 = f32[2,128,1,16,192]{4,3,0,1,2:T(8,128)S(1)} fusion(f32[128]{0:T(128)S(1)} %get-tuple-element.104, f32[128]{0:T(128)S(1)} %get-tuple-element.105, f32[128]{0:T(128)S(1)} %get-tuple-element.106, f32[128]{0:T(128)S(1)} %get-tuple-element.103, s32[128]{0:T(128)S(1)} %get-tuple-element.100, s32[192,128]{1,0:T(8,128)S(1)} %subtract_add_fusion.3, ...), kind=kOutput, calls=%fused_computation.57 | convolution fusion | flops 1249378304 | bytes 5343744 | tf_op jit(solution)/shard_map/czrtx,zjx->czrtj/dot_general | solution.py:163
  242.6 4.0 %fusion.48 = f32[2,128,1,16,128]{4,3,0,1,2:T(8,128)S(1)} fusion(f32[2,128,1,16,128]{4,3,0,1,2:T(8,128)S(1)} %divide_subtract_fusion, f32[2,128,1,15,32]{4,3,0,1,2:T(8,128)S(1)} %get-tuple-element.25, f32[2,128,1,15,32]{4,3,0,1,2:T(8,128)S(1)} %get-tuple-element.24, f32[2,128,1,16,192]{4,3,0,1,2:T(8,128)S(1)} %fusion.39, ...), kind=kLoop, calls=%fused_computation.64 | loop fusion | flops 13107200 | bytes 12451840 | tf_op jit(solution)/shard_map/sub | solution.py:172
  246.6 1.9 copy.258
  248.5 35.5 %all_to_all.49 = f32[2,128,1,2048]{1,0,2,3:T(2,128)S(1)} all-to-all(f32[2,128,1,2048]{1,0,2,3:T(2,128)} %bitcast.604), channel_id=1, replica_groups=mesh['depth'=8,'lat'=16] {'lat'}, dimensions={3} | all-to-all | bytes 4194304 | tf_op jit(solution)/shard_map/all_to_all | solution.py:174
  284.0 1.6 fusion.265
  285.6 1.4 copy.250
  287.0 1.4 copy.249
  (78 shorter events, 13.7 us)
Async XLA Ops:
  0.6 15.2 %copy-start = (f32[8,4]{0,1:T(4,128)S(1)}, f32[8,4]{0,1:T(4,128)}, u32[]{:S(2)}) copy-start(f32[8,4]{0,1:T(4,128)} %param.11) | copy-start | bytes 388
  7.0 8.1 %copy-start.6 = (f32[3,16,128]{2,1,0:T(8,128)S(1)}, f32[3,16,128]{2,1,0:T(8,128)}, u32[]{:S(2)}) copy-start(f32[3,16,128]{2,1,0:T(8,128)} %param.8) | copy-start | bytes 73732
  7.0 8.8 %copy-start.7 = (s32[3,128]{1,0:T(4,128)S(1)}, s32[3,128]{1,0:T(4,128)}, u32[]{:S(2)}) copy-start(s32[3,128]{1,0:T(4,128)} %param.9) | copy-start | bytes 4612
  7.0 8.8 %copy-start.8 = (s32[3,128]{1,0:T(4,128)S(1)}, s32[3,128]{1,0:T(4,128)}, u32[]{:S(2)}) copy-start(s32[3,128]{1,0:T(4,128)} %param.10) | copy-start | bytes 4612
  7.0 39.9 %all-to-all-start = ((f32[2,128,16,128]{3,0,1,2:T(2,128)}), f32[2,128,16,128]{3,0,1,2:T(2,128)S(1)}, u32[]{:S(2)}, u32[]{:S(2)}) async-start(f32[2,128,16,128]{3,0,1,2:T(2,128)} %pad_maximum_fusion), calls=%async_computation | async-start | bytes 4194304 | tf_op jit(solution)/shard_map/all_to_all | solution.py:128
  46.9 5.7 %copy-start.2 = (f32[2,128,16,128]{3,0,1,2:T(2,128)}, f32[2,128,16,128]{3,0,1,2:T(2,128)S(1)}, u32[]{:S(2)}) copy-start(f32[2,128,16,128]{3,0,1,2:T(2,128)S(1)} %all-to-all-done) | copy-start | bytes 6291460
  46.9 24.8 %all-to-all-start.2 = ((f32[1,3,16,128]{3,0,1,2:T(1,128)}), f32[1,3,16,128]{3,0,1,2:T(1,128)S(1)}, u32[]{:S(2)}, u32[]{:S(2)}) async-start(f32[1,3,16,128]{3,0,1,2:T(1,128)} %copy.206), calls=%async_computation.2 | async-start | bytes 49152 | tf_op jit(solution)/shard_map/all_to_all | solution.py:129
  72.4 10.6 %all-to-all-start.1 = ((f32[8,32,128]{2,1,0:T(8,128)}), f32[8,32,128]{2,1,0:T(8,128)S(1)}, u32[]{:S(2)}, u32[]{:S(2)}) async-start(f32[8,32,128]{2,1,0:T(8,128)} %broadcast_in_dim.227), calls=%async_computation.1 | async-start | bytes 262144 | tf_op jit(solution)/shard_map/all_to_all | solution.py:17
  112.6 1.6 copy-start.3
  138.2 9.4 %all-to-all-start.3 = ((f32[8,32,128]{2,1,0:T(8,128)}), f32[8,32,128]{2,1,0:T(8,128)S(1)}, u32[]{:S(2)}, u32[]{:S(2)}) async-start(f32[8,32,128]{2,1,0:T(8,128)} %broadcast_in_dim.239), calls=%async_computation.3 | async-start | bytes 262144 | tf_op jit(solution)/shard_map/all_to_all | solution.py:17
  177.3 1.6 copy-start.4
  177.4 2.2 copy-start.5
  284.0 4.4 %copy-start.1 = (f32[8,4]{0,1:T(4,128)S(1)}, f32[8,4]{0,1:T(4,128)}, u32[]{:S(2)}) copy-start(f32[8,4]{0,1:T(4,128)} %param.11) | copy-start | bytes 388
where the time goes:
time: 292 us; the launch traced here: 289 us
  matrix products  134 us (46%)
  blocking collectives  44.2 us (15%)
  waiting for transfers between devices  42.4 us (15%)
  other arithmetic  27.7 us (9%)
  local copies, waits for them, and re-layouts  19.7 us (7%)
  starting transfers between devices  19.6 us (7%)
    dot_general x3, matrix products, body(): jnp.einsum('czrtx,zjx->czrtj', jnp.stack([grad_color, grad_density]), ban...  80 us
    dot_general x3, matrix products, body(): jnp.einsum('czrtj,zjx->czrtx', with_margins(fields), banded, precision=HI...  52.9 us
    all_to_all x1, blocking collectives, body(): lax.all_to_all(fields, 'lat', split_axis=3, concat_axis=2, tiled=True)  35.5 us
    all_to_all x1, waiting for transfers between devices, body(): lax.all_to_all(fields, 'lat', split_axis=2, concat_axis=3, tiled=True)  30.3 us
    sub x3, other arithmetic, body(): fields - LEARN_RATE * scaled_first / (jnp.sqrt(scaled_second) + ADAM_EPSI...  12.4 us
    all_to_all x2, waiting for transfers between devices, copy_for_each(): lax.all_to_all(jnp.broadcast_to(x[None], (devices, *x.shape)), axis, 0, 0...  12.1 us
    all_to_all x1, blocking collectives, copy_for_each(): lax.all_to_all(jnp.broadcast_to(x[None], (devices, *x.shape)), axis, 0, 0...  8.7 us
    all_to_all x1, starting transfers between devices, body(): lax.all_to_all(fields, 'lat', split_axis=2, concat_axis=3, tiled=True)  8.12 us
  transfers between devices with their start and end apart: 4, of which 3 were waited for; matrix products, arithmetic and copies ran while one was open for 8% of the time, Pallas kernels for 0%

commit v1 on v0

--- a/solution.py
+++ b/solution.py
@@ -171,7 +171,10 @@
         scaled_second = second_moment / (1.0 - BETA_SECOND**step_number)
         fields = fields - LEARN_RATE * scaled_first / (jnp.sqrt(scaled_second) + ADAM_EPSILON)
     fields = fields.reshape(fields.shape[:3] + (fields.shape[3] * tile_width,))
-    fields = lax.all_to_all(fields, "lat", split_axis=3, concat_axis=2, tiled=True)
+    fields = jnp.concatenate(
+        lax.all_to_all(jnp.stack(jnp.split(fields, lax.axis_size("lat"), axis=3)), "lat", 0, 0),
+        axis=2,
+    )
     return (fields[0], fields[1])
 
 

time: 292 us -> 292 us (level)
    unnamed x22 -> x39, local copies, waits for them, and re-layouts: 8.02 us -> 7.47 us
where the time goes in v1:
time: 292 us; the launch traced here: 289 us
  matrix products  134 us (46%)
  blocking collectives  44 us (15%)
  waiting for transfers between devices  42.4 us (15%)
  other arithmetic  27.7 us (9%)
  local copies, waits for them, and re-layouts  19.8 us (7%)
  starting transfers between devices  19.6 us (7%)
    dot_general x3, matrix products, body(): jnp.einsum('czrtx,zjx->czrtj', jnp.stack([grad_color, grad_density]), ban...  80 us
    dot_general x3, matrix products, body(): jnp.einsum('czrtj,zjx->czrtx', with_margins(fields), banded, precision=HI...  52.9 us
    all_to_all x1, blocking collectives, body(): lax.all_to_all(jnp.stack(jnp.split(fields, lax.axis_size('lat'), axis=3))...  35.3 us
    all_to_all x1, waiting for transfers between devices, body(): lax.all_to_all(fields, 'lat', split_axis=2, concat_axis=3, tiled=True)  30.3 us
    sub x3, other arithmetic, body(): fields - LEARN_RATE * scaled_first / (jnp.sqrt(scaled_second) + ADAM_EPSI...  12.4 us
    all_to_all x2, waiting for transfers between devices, copy_for_each(): lax.all_to_all(jnp.broadcast_to(x[None], (devices, *x.shape)), axis, 0, 0...  12.1 us
    all_to_all x1, blocking collectives, copy_for_each(): lax.all_to_all(jnp.broadcast_to(x[None], (devices, *x.shape)), axis, 0, 0...  8.7 us
    all_to_all x1, starting transfers between devices, body(): lax.all_to_all(fields, 'lat', split_axis=2, concat_axis=3, tiled=True)  8.12 us
  transfers between devices with their start and end apart: 4, of which 3 were waited for; matrix products, arithmetic and copies ran while one was open for 8% of the time, Pallas kernels for 0%

profile of v1, /device:TPU:0, one launch (start us, length us, event | category | flops | bytes accessed | tf_op | source)
XLA Modules:
  0.0 288.8 jit_solution(6395481755524939896)
XLA Ops:
  0.7 1.7 copy.256
  2.7 3.2 %pad_maximum_fusion = f32[2,128,16,128]{3,0,1,2:T(2,128)} fusion(f32[1,128,16,128]{3,0,1,2:T(1,128)S(1)} %bitcast.672, f32[1,128,16,128]{3,0,1,2:T(1,128)S(1)} %bitcast.671), kind=kLoop, calls=%fused_computation.74 | loop fusion | flops 524288 | bytes 4194304 | tf_op jit(solution)/shard_map/stack | solution.py:125
  5.9 8.1 %all-to-all-start = ((f32[2,128,16,128]{3,0,1,2:T(2,128)}), f32[2,128,16,128]{3,0,1,2:T(2,128)S(1)}, u32[]{:S(2)}, u32[]{:S(2)}) async-start(f32[2,128,16,128]{3,0,1,2:T(2,128)} %pad_maximum_fusion), calls=%async_computation | async-start | bytes 4194304 | tf_op jit(solution)/shard_map/all_to_all | solution.py:128
  15.5 30.3 %all-to-all-done = f32[2,128,16,128]{3,0,1,2:T(2,128)S(1)} async-done(((f32[2,128,16,128]{3,0,1,2:T(2,128)}), f32[2,128,16,128]{3,0,1,2:T(2,128)S(1)}, u32[]{:S(2)}, u32[]{:S(2)}) %all-to-all-start) | async-done | bytes 2097184 | tf_op jit(solution)/shard_map/all_to_all | solution.py:128
  45.8 3.7 %all-to-all-start.2 = ((f32[1,3,16,128]{3,0,1,2:T(1,128)}), f32[1,3,16,128]{3,0,1,2:T(1,128)S(1)}, u32[]{:S(2)}, u32[]{:S(2)}) async-start(f32[1,3,16,128]{3,0,1,2:T(1,128)} %copy.263), calls=%async_computation.2 | async-start | bytes 49152 | tf_op jit(solution)/shard_map/all_to_all | solution.py:129
  49.5 1.2 copy.411
  51.5 17.9 %fusion.58 = f32[2,128,1,16,128]{4,3,0,1,2:T(8,128)S(1)} fusion(f32[2,128,1,15,32]{4,3,0,1,2:T(8,128)S(1)} %get-tuple-element.53, f32[2,128,1,15,32]{4,3,0,1,2:T(8,128)S(1)} %get-tuple-element.52, f32[2,128,1,16,128]{4,3,0,1,2:T(8,128)S(1)} %bitcast.669, f32[128]{0:T(128)S(1)} %get-tuple-element.131, f32[128]{0:T(128)S(1)} %get-tuple-element.132, ...), kind=kOutput, calls=%fused_computation.91 | convolution fusion | flops 1253572608 | bytes 5278208 | tf_op jit(solution)/shard_map/czrtj,zjx->czrtx/dot_general | solution.py:138
  69.4 1.2 fusion.141
  71.3 4.5 %all-to-all-start.1 = ((f32[8,32,128]{2,1,0:T(8,128)}), f32[8,32,128]{2,1,0:T(8,128)S(1)}, u32[]{:S(2)}, u32[]{:S(2)}) async-start(f32[8,32,128]{2,1,0:T(8,128)} %broadcast_in_dim.227), calls=%async_computation.1 | async-start | bytes 262144 | tf_op jit(solution)/shard_map/all_to_all | solution.py:17
  75.8 6.1 %all-to-all-done.1 = f32[8,32,128]{2,1,0:T(8,128)S(1)} async-done(((f32[8,32,128]{2,1,0:T(8,128)}), f32[8,32,128]{2,1,0:T(8,128)S(1)}, u32[]{:S(2)}, u32[]{:S(2)}) %all-to-all-start.1) | async-done | bytes 131104 | tf_op jit(solution)/shard_map/all_to_all | solution.py:17
  82.1 1.1 bitcast_multiply_fusion.11
  83.3 1.5 fusion.106
  84.8 26.7 %fusion.33 = f32[2,128,1,16,192]{4,3,0,1,2:T(8,128)S(1)} fusion(f32[128]{0:T(128)S(1)} %get-tuple-element.131, f32[128]{0:T(128)S(1)} %get-tuple-element.132, f32[128]{0:T(128)S(1)} %get-tuple-element.133, f32[128]{0:T(128)S(1)} %get-tuple-element.130, s32[128]{0:T(128)S(1)} %get-tuple-element.117, s32[192,128]{1,0:T(8,128)S(1)} %subtract_add_fusion.3, ...), kind=kOutput, calls=%fused_computation.55 | convolution fusion | flops 1249378304 | bytes 5343744 | tf_op jit(solution)/shard_map/czrtx,zjx->czrtj/dot_general | solution.py:163
  113.1 3.8 %divide_subtract_fusion.1 = (f32[2,128,1,16,128]{4,3,0,1,2:T(8,128)S(1)}, f32[2,128,1,16,128]{4,3,0,1,2:T(8,128)}) fusion(f32[2,128,16,128]{3,0,1,2:T(2,128)S(1)} %copy-done.3, f32[2,128,1,15,32]{4,3,0,1,2:T(8,128)S(1)} %get-tuple-element.29, f32[2,128,1,15,32]{4,3,0,1,2:T(8,128)S(1)} %get-tuple-element.28, f32[2,128,1,16,192]{4,3,0,1,2:T(8,128)S(1)} %fusion.33), kind=kLoop, calls=%fused_computation.90 | loop fusion | flops 4718592 | bytes 9371648 | tf_op jit(solution)/shard_map/sub | solution.py:172
  117.7 17.5 %fusion.63 = f32[2,128,1,16,128]{4,3,1,2,0:T(8,128)S(1)} fusion(f32[128]{0:T(128)S(1)} %get-tuple-element.127, f32[128]{0:T(128)S(1)} %get-tuple-element.128, f32[128]{0:T(128)S(1)} %get-tuple-element.129, f32[128]{0:T(128)S(1)} %get-tuple-element.126, s32[128]{0:T(128)S(1)} %get-tuple-element.118, s32[192,128]{1,0:T(8,128)S(1)} %subtract_add_fusion.3, ...), kind=kOutput, calls=%fused_computation.92 | convolution fusion | flops 1253572608 | bytes 5278208 | tf_op jit(solution)/shard_map/czrtj,zjx->czrtx/dot_general | solution.py:138
  135.2 1.2 fusion.92
  137.1 3.4 %all-to-all-start.3 = ((f32[8,32,128]{2,1,0:T(8,128)}), f32[8,32,128]{2,1,0:T(8,128)S(1)}, u32[]{:S(2)}, u32[]{:S(2)}) async-start(f32[8,32,128]{2,1,0:T(8,128)} %broadcast_in_dim.239), calls=%async_computation.3 | async-start | bytes 262144 | tf_op jit(solution)/shard_map/all_to_all | solution.py:17
  140.5 6.0 %all-to-all-done.3 = f32[8,32,128]{2,1,0:T(8,128)S(1)} async-done(((f32[8,32,128]{2,1,0:T(8,128)}), f32[8,32,128]{2,1,0:T(8,128)S(1)}, u32[]{:S(2)}, u32[]{:S(2)}) %all-to-all-start.3) | async-done | bytes 131104 | tf_op jit(solution)/shard_map/all_to_all | solution.py:17
  147.9 1.5 fusion.74
  149.4 26.8 %fusion.36 = f32[2,128,1,16,192]{4,3,0,1,2:T(8,128)S(1)} fusion(f32[128]{0:T(128)S(1)} %get-tuple-element.127, f32[128]{0:T(128)S(1)} %get-tuple-element.128, f32[128]{0:T(128)S(1)} %get-tuple-element.129, f32[128]{0:T(128)S(1)} %get-tuple-element.126, s32[128]{0:T(128)S(1)} %get-tuple-element.118, s32[192,128]{1,0:T(8,128)S(1)} %subtract_add_fusion.3, ...), kind=kOutput, calls=%fused_computation.56 | convolution fusion | flops 1249378304 | bytes 5343744 | tf_op jit(solution)/shard_map/czrtx,zjx->czrtj/dot_general | solution.py:163
  178.5 4.6 %divide_subtract_fusion = f32[2,128,1,16,128]{4,3,0,1,2:T(8,128)S(1)} fusion(f32[2,128,1,16,128]{4,3,0,1,2:T(8,128)S(1)} %copy-done.5, f32[2,128,1,15,32]{4,3,0,1,2:T(8,128)S(1)} %get-tuple-element.27, f32[2,128,1,15,32]{4,3,0,1,2:T(8,128)S(1)} %get-tuple-element.26, f32[2,128,1,16,192]{4,3,0,1,2:T(8,128)S(1)} %fusion.36, f32[2,128,16,128]{3,0,1,2:T(2,128)S(1)} %copy-done.4), kind=kLoop, calls=%fused_computation.88 | loop fusion | flops 11010048 | bytes 9371648 | tf_op jit(solution)/shard_map/sub | solution.py:172
  183.9 17.5 %fusion.68 = f32[2,128,1,16,128]{4,3,1,2,0:T(8,128)S(1)} fusion(f32[128]{0:T(128)S(1)} %get-tuple-element.120, f32[128]{0:T(128)S(1)} %get-tuple-element.121, f32[128]{0:T(128)S(1)} %get-tuple-element.122, f32[128]{0:T(128)S(1)} %get-tuple-element.119, s32[128]{0:T(128)S(1)} %get-tuple-element.116, s32[192,128]{1,0:T(8,128)S(1)} %subtract_add_fusion.3, ...), kind=kOutput, calls=%fused_computation.93 | convolution fusion | flops 1253572608 | bytes 5278208 | tf_op jit(solution)/shard_map/czrtj,zjx->czrtx/dot_general | solution.py:138
  201.3 1.2 fusion.86
  202.6 8.7 %all_to_all.44 = f32[8,32,128]{2,1,0:T(8,128)S(1)} all-to-all(f32[8,32,128]{2,1,0:T(8,128)S(1)} %broadcast_in_dim.248), channel_id=1, replica_groups=mesh['depth'=8,'lat'=16] {'depth'}, dimensions={0} | all-to-all | bytes 262144 | tf_op jit(solution)/shard_map/all_to_all | solution.py:17
  212.7 1.5 fusion.77
  214.2 26.5 %fusion.39 = f32[2,128,1,16,192]{4,3,0,1,2:T(8,128)S(1)} fusion(f32[128]{0:T(128)S(1)} %get-tuple-element.120, f32[128]{0:T(128)S(1)} %get-tuple-element.121, f32[128]{0:T(128)S(1)} %get-tuple-element.122, f32[128]{0:T(128)S(1)} %get-tuple-element.119, s32[128]{0:T(128)S(1)} %get-tuple-element.116, s32[192,128]{1,0:T(8,128)S(1)} %subtract_add_fusion.3, ...), kind=kOutput, calls=%fused_computation.57 | convolution fusion | flops 1249378304 | bytes 5343744 | tf_op jit(solution)/shard_map/czrtx,zjx->czrtj/dot_general | solution.py:163
  241.5 4.0 %fusion.48 = f32[2,128,1,16,128]{4,3,0,1,2:T(8,128)S(1)} fusion(f32[2,128,1,16,128]{4,3,0,1,2:T(8,128)S(1)} %divide_subtract_fusion, f32[2,128,1,15,32]{4,3,0,1,2:T(8,128)S(1)} %get-tuple-element.25, f32[2,128,1,15,32]{4,3,0,1,2:T(8,128)S(1)} %get-tuple-element.24, f32[2,128,1,16,192]{4,3,0,1,2:T(8,128)S(1)} %fusion.39, ...), kind=kLoop, calls=%fused_computation.64 | loop fusion | flops 13107200 | bytes 12451840 | tf_op jit(solution)/shard_map/sub | solution.py:172
  245.5 2.1 reshape.865
  247.6 1.9 fusion.281
  249.8 35.3 %all_to_all.45 = f32[16,2,128,1,128]{4,2,3,1,0:T(8,128)S(1)} all-to-all(f32[16,2,128,1,128]{4,2,3,1,0:T(8,128)S(1)} %fusion.166), channel_id=1, replica_groups=mesh['depth'=8,'lat'=16] {'lat'}, dimensions={0} | all-to-all | bytes 4194304 | tf_op jit(solution)/shard_map/all_to_all | solution.py:175
  285.3 1.6 copy.320
  286.9 1.6 copy.319
  (97 shorter events, 13.3 us)
Async XLA Ops:
  0.6 14.1 %copy-start = (f32[8,4]{0,1:T(4,128)S(1)}, f32[8,4]{0,1:T(4,128)}, u32[]{:S(2)}) copy-start(f32[8,4]{0,1:T(4,128)} %param.11) | copy-start | bytes 388
  0.6 1.7 copy-start.6
  5.9 8.1 %copy-start.7 = (f32[3,16,128]{2,1,0:T(8,128)S(1)}, f32[3,16,128]{2,1,0:T(8,128)}, u32[]{:S(2)}) copy-start(f32[3,16,128]{2,1,0:T(8,128)} %param.8) | copy-start | bytes 73732
  5.9 8.8 %copy-start.8 = (s32[3,128]{1,0:T(4,128)S(1)}, s32[3,128]{1,0:T(4,128)}, u32[]{:S(2)}) copy-start(s32[3,128]{1,0:T(4,128)} %param.9) | copy-start | bytes 4612
  5.9 8.8 %copy-start.9 = (s32[3,128]{1,0:T(4,128)S(1)}, s32[3,128]{1,0:T(4,128)}, u32[]{:S(2)}) copy-start(s32[3,128]{1,0:T(4,128)} %param.10) | copy-start | bytes 4612
  5.9 39.9 %all-to-all-start = ((f32[2,128,16,128]{3,0,1,2:T(2,128)}), f32[2,128,16,128]{3,0,1,2:T(2,128)S(1)}, u32[]{:S(2)}, u32[]{:S(2)}) async-start(f32[2,128,16,128]{3,0,1,2:T(2,128)} %pad_maximum_fusion), calls=%async_computation | async-start | bytes 4194304 | tf_op jit(solution)/shard_map/all_to_all | solution.py:128
  45.8 4.9 %copy-start.2 = (f32[2,128,16,128]{3,0,1,2:T(2,128)}, f32[2,128,16,128]{3,0,1,2:T(2,128)S(1)}, u32[]{:S(2)}) copy-start(f32[2,128,16,128]{3,0,1,2:T(2,128)S(1)} %all-to-all-done) | copy-start | bytes 6291460
  45.8 24.8 %all-to-all-start.2 = ((f32[1,3,16,128]{3,0,1,2:T(1,128)}), f32[1,3,16,128]{3,0,1,2:T(1,128)S(1)}, u32[]{:S(2)}, u32[]{:S(2)}) async-start(f32[1,3,16,128]{3,0,1,2:T(1,128)} %copy.263), calls=%async_computation.2 | async-start | bytes 49152 | tf_op jit(solution)/shard_map/all_to_all | solution.py:129
  71.3 10.6 %all-to-all-start.1 = ((f32[8,32,128]{2,1,0:T(8,128)}), f32[8,32,128]{2,1,0:T(8,128)S(1)}, u32[]{:S(2)}, u32[]{:S(2)}) async-start(f32[8,32,128]{2,1,0:T(8,128)} %broadcast_in_dim.227), calls=%async_computation.1 | async-start | bytes 262144 | tf_op jit(solution)/shard_map/all_to_all | solution.py:17
  111.5 1.6 copy-start.3
  137.1 9.4 %all-to-all-start.3 = ((f32[8,32,128]{2,1,0:T(8,128)}), f32[8,32,128]{2,1,0:T(8,128)S(1)}, u32[]{:S(2)}, u32[]{:S(2)}) async-start(f32[8,32,128]{2,1,0:T(8,128)} %broadcast_in_dim.239), calls=%async_computation.3 | async-start | bytes 262144 | tf_op jit(solution)/shard_map/all_to_all | solution.py:17
  176.2 1.6 copy-start.4
  176.3 2.2 copy-start.5
  285.3 3.2 %copy-start.1 = (f32[8,4]{0,1:T(4,128)S(1)}, f32[8,4]{0,1:T(4,128)}, u32[]{:S(2)}) copy-start(f32[8,4]{0,1:T(4,128)} %param.11) | copy-start | bytes 388
